TPU v7x, 32 devices: a whole 2x2x4 slice. The times are simulated.
32 devices in a mesh: seq: 4 (over z), shard: 8 (over y, x, core).
Axes of the slice: x: 2, y: 2, z: 4, core: 2. Of those that a mesh axis runs over, the one named last changes fastest.
Arguments:
- tokens: bfloat16 [8, 2048, 1024], P('shard', 'seq'), may hold values from -6 to 6
- ln1_gain: bfloat16 [1024], P(('seq', 'shard')), may hold values from 0.5 to 1.5
- ln1_bias: bfloat16 [1024], P(('seq', 'shard')), may hold values from -3 to 3
- w_qkv: bfloat16 [1024, 3072], P(('seq', 'shard')), may hold values from -0.1875 to 0.1875
- bias_query: bfloat16 [1024], P(('seq', 'shard')), may hold values from -3 to 3
- bias_value: bfloat16 [1024], P(('seq', 'shard')), may hold values from -3 to 3
- w_out: bfloat16 [1024, 1024], P(('seq', 'shard')), may hold values from -1 to 1
- bias_out: bfloat16 [1024], P(('seq', 'shard')), may hold values from -3 to 3
- ln2_gain: bfloat16 [1024], P(('seq', 'shard')), may hold values from 0.5 to 1.5
- ln2_bias: bfloat16 [1024], P(('seq', 'shard')), may hold values from -3 to 3
- w_in: bfloat16 [1024, 4096], P(('seq', 'shard')), may hold values from -0.1875 to 0.1875
- bias_in: bfloat16 [4096], P(('seq', 'shard')), may hold values from -3 to 3
- w_back: bfloat16 [4096, 1024], P(('seq', 'shard')), may hold values from -0.09375 to 0.09375
- bias_back: bfloat16 [1024], P(('seq', 'shard')), may hold values from -3 to 3
- cotangent: bfloat16 [8, 2048, 1024], P('shard', 'seq'), may hold values from -6 to 6
Outputs:
- result: bfloat16 [8, 2048, 1024], P('shard', 'seq')
- grad_tokens: float32 [8, 2048, 1024], P('shard', 'seq')
- grad_ln1_gain: float32 [1024], P(('seq', 'shard'))
- grad_ln1_bias: float32 [1024], P(('seq', 'shard'))
- grad_w_qkv: float32 [1024, 3072], P(('seq', 'shard'))
- grad_bias_query: float32 [1024], P(('seq', 'shard'))
- grad_bias_value: float32 [1024], P(('seq', 'shard'))
- grad_w_out: float32 [1024, 1024], P(('seq', 'shard'))
- grad_bias_out: float32 [1024], P(('seq', 'shard'))
- grad_ln2_gain: float32 [1024], P(('seq', 'shard'))
- grad_ln2_bias: float32 [1024], P(('seq', 'shard'))
- grad_w_in: float32 [1024, 4096], P(('seq', 'shard'))
- grad_bias_in: float32 [4096], P(('seq', 'shard'))
- grad_w_back: float32 [4096, 1024], P(('seq', 'shard'))
- grad_bias_back: float32 [1024], P(('seq', 'shard'))
All inputs are finite; a program needn't handle non-finite values.
Results may differ from a plain program's by a relative error of at most 0.014.
The roundings to bfloat16 on the way count: a program that leaves them out, or rounds other values in their place, can miss the bound.
Values may be sent and summed in bfloat16 or wider, within the bound.
A program may use at most 192 MiB of HBM per device.

v0:
```python
import math
import jax
import jax.numpy as jnp
from jax import lax
from jax.sharding import PartitionSpec as P

HEAD_DIM = 64
norm_eps = 1e-05
gelu_c = math.sqrt(2.0 / math.pi)


def normalize(values):
    mean_row = jnp.mean(values, axis=-1, keepdims=True)
    centred = values - mean_row
    var_row = jnp.mean(centred * centred, axis=-1, keepdims=True)
    scale_row = lax.rsqrt(var_row + norm_eps)
    return (centred * scale_row, scale_row)


def norm_back(dnormed, normed, scale_row):
    return scale_row * (
        dnormed
        - jnp.mean(dnormed, axis=-1, keepdims=True)
        - normed * jnp.mean(dnormed * normed, axis=-1, keepdims=True)
    )


def gelu_pair(inputs):
    inner = gelu_c * (inputs + 0.044715 * inputs * inputs * inputs)
    tanh_val = jnp.tanh(inner)
    value = 0.5 * inputs * (1.0 + tanh_val)
    slope = 0.5 * (1.0 + tanh_val) + 0.5 * inputs * (1.0 - tanh_val * tanh_val) * gelu_c * (
        1.0 + 3.0 * 0.044715 * inputs * inputs
    )
    return (value, slope)


def masked_scores(query_block, keys, start, scale):
    block = query_block.shape[0]
    length = keys.shape[0]
    scores = (
        jnp.einsum("qgd,kgd->gqk", query_block, keys, preferred_element_type=jnp.float32) * scale
    )
    q_pos = start + jnp.arange(block, dtype=jnp.int32)
    k_pos = jnp.arange(length, dtype=jnp.int32)
    allowed = k_pos[None, None, :] <= q_pos[None, :, None]
    return jnp.where(allowed, scores, -1e30)


def attend_forward(query, keys, values):
    length, groups, width = query.shape
    block = min(512, length)
    scale = 1.0 / math.sqrt(width)

    def one_block(index):
        start = index * block
        q_blk = lax.dynamic_slice_in_dim(query, start, block, 0)
        scores = masked_scores(q_blk, keys, start, scale)
        log_total = jnp.log(jnp.sum(jnp.exp(scores), axis=-1))
        probs = jnp.exp(scores - log_total[:, :, None]).astype(jnp.bfloat16)
        attended = jnp.einsum("gqk,kgd->qgd", probs, values, preferred_element_type=jnp.float32)
        return (attended.astype(jnp.bfloat16), log_total)

    outs, logs = lax.map(one_block, jnp.arange(length // block, dtype=jnp.int32))
    return (outs.reshape(length, groups, width), logs)


def attend_backward(query, keys, values, attended, logs, d_att):
    length, groups, width = query.shape
    block = min(512, length)
    scale = 1.0 / math.sqrt(width)

    def one_block(carry, index):
        d_keys, d_values = carry
        start = index * block
        q_blk = lax.dynamic_slice_in_dim(query, start, block, 0)
        o_blk = lax.dynamic_slice_in_dim(attended, start, block, 0)
        do_blk = lax.dynamic_slice_in_dim(d_att, start, block, 0)
        scores = masked_scores(q_blk, keys, start, scale)
        log_total = lax.dynamic_index_in_dim(logs, index, 0, keepdims=False)
        probs = jnp.exp(scores - log_total[:, :, None])
        probs_b = probs.astype(jnp.bfloat16)
        d_values = d_values + jnp.einsum(
            "gqk,qgd->kgd", probs_b, do_blk, preferred_element_type=jnp.float32
        )
        d_probs = jnp.einsum("qgd,kgd->gqk", do_blk, values, preferred_element_type=jnp.float32)
        delta = jnp.swapaxes(
            jnp.sum(do_blk.astype(jnp.float32) * o_blk.astype(jnp.float32), axis=-1), 0, 1
        )
        d_scores = (probs * (d_probs - delta[:, :, None]) * scale).astype(jnp.bfloat16)
        d_query = jnp.einsum(
            "gqk,kgd->qgd", d_scores, keys, preferred_element_type=jnp.float32
        ).astype(jnp.bfloat16)
        d_keys = d_keys + jnp.einsum(
            "gqk,qgd->kgd", d_scores, q_blk, preferred_element_type=jnp.float32
        )
        return ((d_keys, d_values), d_query)

    zeros = jnp.zeros((length, groups, width), jnp.float32)
    (d_keys, d_values), d_queries = lax.scan(
        one_block, (zeros, zeros), jnp.arange(length // block, dtype=jnp.int32)
    )
    return (
        d_queries.reshape(length, groups, width),
        d_keys.astype(jnp.bfloat16),
        d_values.astype(jnp.bfloat16),
    )


def col_dot(left, right):
    return lax.dot_general(
        left, right, (((0,), (0,)), ((), ())), preferred_element_type=jnp.float32
    )


def row_dot(left, right):
    return lax.dot_general(
        left, right, (((1,), (1,)), ((), ())), preferred_element_type=jnp.float32
    )


def per_device(
    tokens,
    ln1_gain,
    ln1_bias,
    w_qkv,
    bias_query,
    bias_value,
    w_out,
    bias_out,
    ln2_gain,
    ln2_bias,
    w_in,
    bias_in,
    w_back,
    bias_back,
    cotangent,
):
    f32 = jnp.float32
    params = (
        lax.all_gather(ln1_gain, ("seq", "shard"), axis=0, tiled=True),
        lax.all_gather(ln1_bias, ("seq", "shard"), axis=0, tiled=True),
        lax.all_gather(w_qkv, ("seq", "shard"), axis=0, tiled=True),
        lax.all_gather(bias_query, ("seq", "shard"), axis=0, tiled=True),
        lax.all_gather(bias_value, ("seq", "shard"), axis=0, tiled=True),
        lax.all_gather(w_out, ("seq", "shard"), axis=0, tiled=True),
        lax.all_gather(bias_out, ("seq", "shard"), axis=0, tiled=True),
        lax.all_gather(ln2_gain, ("seq", "shard"), axis=0, tiled=True),
        lax.all_gather(ln2_bias, ("seq", "shard"), axis=0, tiled=True),
        lax.all_gather(w_in, ("seq", "shard"), axis=0, tiled=True),
        lax.all_gather(bias_in, ("seq", "shard"), axis=0, tiled=True),
        lax.all_gather(w_back, ("seq", "shard"), axis=0, tiled=True),
        lax.all_gather(bias_back, ("seq", "shard"), axis=0, tiled=True),
    )
    (
        g_one,
        s_one,
        full_qkv,
        full_bq,
        full_bv,
        full_out,
        full_bo,
        g_two,
        s_two,
        full_in,
        full_bin,
        full_back,
        full_bback,
    ) = params
    rows = tokens.shape[1]
    width = tokens.shape[2]
    x_f = tokens[0].astype(f32)
    normed1, scale1 = normalize(x_f)
    h_one = (normed1 * g_one.astype(f32) + s_one.astype(f32)).astype(jnp.bfloat16)
    bias_qkv = jnp.concatenate([full_bq.astype(f32), jnp.zeros((width,), f32), full_bv.astype(f32)])
    qkv = (jnp.dot(h_one, full_qkv, preferred_element_type=f32) + bias_qkv).astype(jnp.bfloat16)
    grouped = lax.all_to_all(
        qkv.reshape(rows, 3, width), "seq", split_axis=2, concat_axis=0, tiled=True
    )
    length = grouped.shape[0]
    local_width = grouped.shape[2]
    groups = local_width // HEAD_DIM
    query = grouped[:, 0].reshape(length, groups, HEAD_DIM)
    keys = grouped[:, 1].reshape(length, groups, HEAD_DIM)
    values = grouped[:, 2].reshape(length, groups, HEAD_DIM)
    attended, logs = attend_forward(query, keys, values)
    att_tok = lax.all_to_all(
        attended.reshape(length, local_width), "seq", split_axis=0, concat_axis=1, tiled=True
    )
    resid = x_f + jnp.dot(att_tok, full_out, preferred_element_type=f32) + full_bo.astype(f32)
    normed2, scale2 = normalize(resid)
    h_two = (normed2 * g_two.astype(f32) + s_two.astype(f32)).astype(jnp.bfloat16)
    pre = jnp.dot(h_two, full_in, preferred_element_type=f32) + full_bin.astype(f32)
    act_val, slope = gelu_pair(pre)
    act = act_val.astype(jnp.bfloat16)
    result = (
        resid + jnp.dot(act, full_back, preferred_element_type=f32) + full_bback.astype(f32)
    ).astype(jnp.bfloat16)
    cot_b = cotangent[0]
    cot_f = cot_b.astype(f32)
    g_w_back = col_dot(act, cot_b)
    g_b_back = jnp.sum(cot_f, axis=0)
    d_pre = (row_dot(cot_b, full_back) * slope).astype(jnp.bfloat16)
    g_w_in = col_dot(h_two, d_pre)
    g_b_in = jnp.sum(d_pre.astype(f32), axis=0)
    d_h2 = row_dot(d_pre, full_in)
    g_g2 = jnp.sum(d_h2 * normed2, axis=0)
    g_s2 = jnp.sum(d_h2, axis=0)
    d_resid = cot_f + norm_back(d_h2 * g_two.astype(f32), normed2, scale2)
    d_resid_b = d_resid.astype(jnp.bfloat16)
    g_w_out = col_dot(att_tok, d_resid_b)
    g_b_out = jnp.sum(d_resid, axis=0)
    d_att_tok = row_dot(d_resid_b, full_out).astype(jnp.bfloat16)
    d_att = lax.all_to_all(d_att_tok, "seq", split_axis=1, concat_axis=0, tiled=True).reshape(
        length, groups, HEAD_DIM
    )
    d_query, d_keys, d_values = attend_backward(query, keys, values, attended, logs, d_att)
    stacked = jnp.stack(
        [
            d_query.reshape(length, local_width),
            d_keys.reshape(length, local_width),
            d_values.reshape(length, local_width),
        ],
        axis=1,
    )
    d_qkv = lax.all_to_all(stacked, "seq", split_axis=0, concat_axis=2, tiled=True).reshape(
        rows, 3 * width
    )
    g_w_qkv = col_dot(h_one, d_qkv)
    g_bq = jnp.sum(d_qkv[:, :width].astype(f32), axis=0)
    g_bv = jnp.sum(d_qkv[:, 2 * width :].astype(f32), axis=0)
    d_h1 = row_dot(d_qkv, full_qkv)
    g_g1 = jnp.sum(d_h1 * normed1, axis=0)
    g_s1 = jnp.sum(d_h1, axis=0)
    d_tokens = d_resid + norm_back(d_h1 * g_one.astype(f32), normed1, scale1)
    summed = (
        lax.psum_scatter(g_g1, ("seq", "shard"), scatter_dimension=0, tiled=True),
        lax.psum_scatter(g_s1, ("seq", "shard"), scatter_dimension=0, tiled=True),
        lax.psum_scatter(g_w_qkv, ("seq", "shard"), scatter_dimension=0, tiled=True),
        lax.psum_scatter(g_bq, ("seq", "shard"), scatter_dimension=0, tiled=True),
        lax.psum_scatter(g_bv, ("seq", "shard"), scatter_dimension=0, tiled=True),
        lax.psum_scatter(g_w_out, ("seq", "shard"), scatter_dimension=0, tiled=True),
        lax.psum_scatter(g_b_out, ("seq", "shard"), scatter_dimension=0, tiled=True),
        lax.psum_scatter(g_g2, ("seq", "shard"), scatter_dimension=0, tiled=True),
        lax.psum_scatter(g_s2, ("seq", "shard"), scatter_dimension=0, tiled=True),
        lax.psum_scatter(g_w_in, ("seq", "shard"), scatter_dimension=0, tiled=True),
        lax.psum_scatter(g_b_in, ("seq", "shard"), scatter_dimension=0, tiled=True),
        lax.psum_scatter(g_w_back, ("seq", "shard"), scatter_dimension=0, tiled=True),
        lax.psum_scatter(g_b_back, ("seq", "shard"), scatter_dimension=0, tiled=True),
    )
    (
        r_g1,
        r_s1,
        r_w_qkv,
        r_bq,
        r_bv,
        r_w_out,
        r_b_out,
        r_g2,
        r_s2,
        r_w_in,
        r_b_in,
        r_w_back,
        r_b_back,
    ) = summed
    return (
        result[None],
        d_tokens[None],
        r_g1,
        r_s1,
        r_w_qkv,
        r_bq,
        r_bv,
        r_w_out,
        r_b_out,
        r_g2,
        r_s2,
        r_w_in,
        r_b_in,
        r_w_back,
        r_b_back,
    )


def solution(mesh):
    return jax.shard_map(
        per_device,
        mesh=mesh,
        in_specs=(
            P("shard", "seq", None),
            P(("seq", "shard")),
            P(("seq", "shard")),
            P(("seq", "shard"), None),
            P(("seq", "shard")),
            P(("seq", "shard")),
            P(("seq", "shard"), None),
            P(("seq", "shard")),
            P(("seq", "shard")),
            P(("seq", "shard")),
            P(("seq", "shard"), None),
            P(("seq", "shard")),
            P(("seq", "shard"), None),
            P(("seq", "shard")),
            P("shard", "seq", None),
        ),
        out_specs=(
            P("shard", "seq", None),
            P("shard", "seq", None),
            P(("seq", "shard")),
            P(("seq", "shard")),
            P(("seq", "shard"), None),
            P(("seq", "shard")),
            P(("seq", "shard")),
            P(("seq", "shard"), None),
            P(("seq", "shard")),
            P(("seq", "shard")),
            P(("seq", "shard")),
            P(("seq", "shard"), None),
            P(("seq", "shard")),
            P(("seq", "shard"), None),
            P(("seq", "shard")),
        ),
        check_vma=False,
    )
```

profile of v0, /device:TPU:13, one launch (start us, length us, event | category | flops | bytes accessed | tf_op | source)
XLA Modules:
  0.0 1236.6 jit_solution(11690931587588916261)
XLA Ops:
  16.1 40.8 %all-reduce.18 = (bf16[1024]{0:T(1024)(128)(2,1)S(1)}, bf16[1024]{0:T(1024)(128)(2,1)S(1)}, bf16[1024]{0:T(1024)(128)(2,1)S(1)}, bf16[1024]{0:T(1024)(128)(2,1)S...) all-reduce(bf16[1024]{0:T(1024)(128)(2,1)S(1)} %dynamic-update-slic, ...), channel_id=1, replica_groups=mesh['seq'=4,'shard'=8] {'seq','shard'}, use_global_device_ids=true, to_apply=%add.3 | all-reduce | flops 8192 | bytes 32768
  60.1 21.6 %all-gather.6.cloned.1.call-done = bf16[1024,3072]{1,0:T(8,128)(2,1)} async-done(((bf16[32,3072]{1,0:T(8,128)(2,1)}), bf16[1024,3072]{1,0:T(8,128)(2,1)}) %all-gather.6.cloned.1.call-update) | async-done | bytes 6291472 | tf_op jit(solution)/shard_map/all_gather | solution.py:143
  81.7 8.4 add_convert_fusion
  97.9 5.0 all-to-all-start
  103.5 101.0 %all-to-all-done = bf16[512,3,1024]{0,1,2:T(4,128)(2,1)} async-done(((bf16[512,3,1024]{0,1,2:T(4,128)(2,1)}), bf16[512,3,1024]{0,1,2:T(4,128)(2,1)}, u32[]{:S(2)}, u32[]{:S(2)}) %all-to-all-start) | async-done | bytes 3145760 | tf_op jit(solution)/shard_map/all_to_all | solution.py:177
  216.3 50.8 %while.27 = (s32[]{:T(128)}, bf16[4,512,4,64]{1,3,2,0:T(8,128)(2,1)}, f32[4,4,512]{2,1,0:T(4,128)}, s32[4]{0:T(128)S(1)}, bf16[2048,4,64]{0,2,1:T(8,128)(2,1)S(1...) while((s32[]{:T(128)}, ...), condition=%wide.region_4.5_spmd, body=%wide.region_2.4_spmd.sunk | while | flops 1104280064 | bytes 43569372 | solution.py:64
  218.2 4.7 exponential_reduce_fusion.2
  222.9 5.5 fusion.127
  230.9 4.7 exponential_reduce_fusion.2
  235.6 5.5 fusion.127
  248.3 5.5 fusion.127
  256.3 4.7 exponential_reduce_fusion.2
  261.0 5.5 fusion.127
  268.1 7.5 all-to-all-start.1
  275.6 54.4 %all-gather = bf16[32,1,128]{2,1,0:T(2,128)(2,1)S(1)} all-gather(bf16[1,1,128]{2,1,0:T(2,128)(2,1)S(1)} %bitcast.188), channel_id=1, replica_groups=mesh['seq'=4,'shard'=8] {'seq','shard'}, dimensions={0}, use_global_device_ids=true | all-gather | bytes 8448 | tf_op jit(solution)/shard_map/all_gather | solution.py:151
  335.1 10.6 fusion.83
  345.7 11.9 all-gather.12.cloned.1.call-done
  357.6 14.9 %convert_reduce_fusion = (f32[4096]{0:T(1024)}, bf16[512,4096]{1,0:T(8,128)(2,1)}) fusion(f32[512,4096]{1,0:T(8,128)} %fusion.83, f32[4096]{0:T(1024)S(1)} %bitcast.185, bf16[4096,1024]{1,0:T(8,128)(2,1)} %all-gather.12.cloned.1.call-done, bf16[1,512,1024]{2,1,0:T(8,128)(2,1)} %param.33), kind=kOutput, calls=%fused_computation.52 | convolution fusion | flops 4341100544 | bytes 22052864 | tf_op jit(solution)/shard_map/dot_general | solution.py:117
  372.5 7.7 multiply_reduce_fusion.1
  397.3 15.6 %all-to-all-done.2 = bf16[512,4,256]{2,0,1:T(8,128)(2,1)} async-done(((bf16[512,4,256]{2,0,1:T(8,128)(2,1)}), bf16[512,4,256]{2,0,1:T(8,128)(2,1)}, u32[]{:S(2)}, u32[]{:S(2)}) %all-to-all-start.2) | async-done | bytes 1048608 | tf_op jit(solution)/shard_map/all_to_all | solution.py:214
  416.7 156.1 %while.28 = (s32[]{:T(128)}, f32[2048,4,64]{0,2,1:T(8,128)}, f32[2048,4,64]{0,2,1:T(8,128)}, bf16[4,512,4,64]{1,3,2,0:T(8,128)(2,1)}, s32[4]{0:T(128)S(1)}, /*in...) while((s32[]{:T(128)}, f32[2048,4,64]{0,2,1:T(8,128)}, ...), condition=%wide.region_11.12_spmd.clone, body=%wide.region_9.11_spmd.clone.sunk | while | flops 2734291456 | bytes 138236336 | solution.py:100
  426.2 7.2 fusion.140
  433.4 10.5 multiply_convert_fusion.5
  443.9 7.0 fusion.141
  464.3 7.6 fusion.140
  471.9 10.5 multiply_convert_fusion.5
  482.4 7.0 fusion.141
  489.4 4.8 fusion.139
  503.4 7.6 fusion.140
  511.0 10.5 multiply_convert_fusion.5
  521.5 6.9 fusion.141
  528.5 4.8 fusion.139
  542.5 7.6 fusion.140
  550.1 10.5 multiply_convert_fusion.5
  560.6 6.9 fusion.141
  567.6 4.8 fusion.139
  578.9 4.8 copy.82
  583.7 97.2 %all_to_all.68 = bf16[2048,3,256]{2,1,0:T(4,128)(2,1)S(1)} all-to-all(bf16[2048,3,256]{2,1,0:T(4,128)(2,1)} %copy.82), channel_id=1, replica_groups=mesh['seq'=4,'shard'=8] {'seq'}, dimensions={0} | all-to-all | bytes 6291456 | tf_op jit(solution)/shard_map/all_to_all | solution.py:226
  683.0 4.8 copy.84
  687.8 8.7 fusion.65
  697.7 16.2 %fusion.68 = f32[4096,1024]{1,0:T(8,128)} fusion(bf16[1,512,1024]{2,1,0:T(8,128)(2,1)S(1)} %copy-done.16, f32[512,4096]{1,0:T(8,128)} %fusion.83, f32[4096]{0:T(1024)S(1)} %bitcast.186), kind=kOutput, calls=%fused_computation.98 | convolution fusion | flops 4315938816 | bytes 26230784 | tf_op jit(solution)/shard_map/dot_general | solution.py:111
  715.7 11.5 fusion.82
  727.8 13.2 %fusion.63 = bf16[1,512,1024]{2,1,0:T(8,128)(2,1)} fusion(f32[512,1024]{1,0:T(8,128)S(1)} %copy-done.6, bf16[4096,1024]{1,0:T(8,128)(2,1)} %all-gather.12.cloned.1.call-done, f32[1024]{0:T(1024)S(1)} %convert_element_type.124, f32[512,4096]{1,0:T(8,128)} %fusion.83, f32[4096]{0:T(1024)S(1)} %bitcast.187), kind=kOutput, calls=%fused_computation.94 | convolution fusion | flops 4317511680 | bytes 19943424 | tf_op jit(solution)/shard_map/dot_general | solution.py:197
  741.5 8.8 fusion.56
  750.3 45.6 %all-reduce.17 = (f32[1024]{0:T(1024)S(1)}, f32[1024]{0:T(1024)S(1)}, f32[1024]{0:T(1024)S(1)}, f32[1024]{0:T(1024)S(1)}, f32[1024]{0:T(1024)S(1)}, /*index=5*/f...) all-reduce(f32[1024]{0:T(1024)S(1)} %get-tuple-element.184, ...), channel_id=2, replica_groups=mesh['seq'=4,'shard'=8] {'seq','shard'}, use_global_device_ids=true, to_apply=%region_15.16.clone | all-reduce | flops 12288 | bytes 98304
  804.8 48.2 %reduce-scatter.5.cloned.1.call-done = f32[32,3072]{1,0:T(8,128)} async-done(((f32[1024,3072]{1,0:T(8,128)}), f32[32,3072]{1,0:T(8,128)}) %reduce-scatter.5.cloned.1.call-update) | async-done | bytes 393232 | tf_op jit(solution)/shard_map/reduce_scatter | solution.py:239
  853.0 189.0 %reduce-scatter.11.cloned.1.call-done = f32[128,1024]{1,0:T(8,128)} async-done(((f32[4096,1024]{1,0:T(8,128)}), f32[128,1024]{1,0:T(8,128)}) %reduce-scatter.11.cloned.1.call-update) | async-done | bytes 524304 | tf_op jit(solution)/shard_map/reduce_scatter | solution.py:248
  1042.1 187.5 %reduce-scatter.9.cloned.1.call-done = f32[32,4096]{1,0:T(8,128)} async-done(((f32[1024,4096]{1,0:T(8,128)}), f32[32,4096]{1,0:T(8,128)}) %reduce-scatter.9.cloned.1.call-update) | async-done | bytes 524304 | tf_op jit(solution)/shard_map/reduce_scatter | solution.py:246
  (270 shorter events, 122.8 us)
Async XLA Ops:
  7.2 74.5 %all-gather.6.cloned.1.call-start = ((), (), s32[]{:S(2)}) async-start(), calls=%async_computation.8 | async-start | bytes 6488064 | tf_op jit(solution)/shard_map/all_gather | solution.py:143
  7.9 322.1 %all-gather.8.cloned.1.call-start = ((), (), s32[]{:S(2)}) async-start(), calls=%async_computation.9 | async-start | bytes 2162688 | tf_op jit(solution)/shard_map/all_gather | solution.py:146
  8.7 326.5 %all-gather.10.cloned.1.call-start = ((), (), s32[]{:S(2)}) async-start(), calls=%async_computation.10 | async-start | bytes 8650752 | tf_op jit(solution)/shard_map/all_gather | solution.py:150
  56.9 24.8 %copy-start.25 = (f32[1024]{0:T(1024)}, f32[1024]{0:T(1024)S(1)}, u32[]{:S(2)}) copy-start(f32[1024]{0:T(1024)S(1)} %convert_element_type.112) | copy-start | bytes 12292
  56.9 24.8 %copy-start.38 = (f32[1024]{0:T(1024)}, f32[1024]{0:T(1024)S(1)}, u32[]{:S(2)}) copy-start(f32[1024]{0:T(1024)S(1)} %convert_element_type.113) | copy-start | bytes 12292
  58.4 23.3 %copy-start.21 = (f32[512]{0:T(512)}, f32[512]{0:T(512)S(1)}, u32[]{:S(2)}) copy-start(f32[512]{0:T(512)S(1)} %broadcast_multiply_fusion.5) | copy-start | bytes 6148
  60.1 21.7 %copy-start.34 = (f32[512]{0:T(512)}, f32[512]{0:T(512)S(1)}, u32[]{:S(2)}) copy-start(f32[512]{0:T(512)S(1)} %add_rsqrt_fusion.1) | copy-start | bytes 6148
  97.9 106.6 %all-to-all-start = ((bf16[512,3,1024]{0,1,2:T(4,128)(2,1)}), bf16[512,3,1024]{0,1,2:T(4,128)(2,1)}, u32[]{:S(2)}, u32[]{:S(2)}) async-start(bf16[512,3,1024]{0,1,2:T(4,128)(2,1)} %copy.72), calls=%async_computation | async-start | bytes 8388608 | tf_op jit(solution)/shard_map/all_to_all | solution.py:177
  103.0 254.6 %all-gather.12.cloned.1.call-start = ((), (), s32[]{:S(2)}) async-start(), calls=%async_computation.11 | async-start | bytes 8650752 | tf_op jit(solution)/shard_map/all_gather | solution.py:152
  216.3 59.3 %copy-start.43 = (bf16[128]{0:T(256)(128)(2,1)S(1)}, bf16[128]{0:T(256)(128)(2,1)}, u32[]{:S(2)}) copy-start(bf16[128]{0:T(256)(128)(2,1)} %param.30) | copy-start | bytes 772
  268.1 61.9 %all-to-all-start.1 = ((bf16[4,512,256]{1,2,0:T(8,128)(2,1)}), bf16[4,512,256]{1,2,0:T(8,128)(2,1)S(1)}, u32[]{:S(2)}, u32[]{:S(2)}) async-start(bf16[4,512,256]{1,2,0:T(8,128)(2,1)} %bitcast.12), calls=%async_computation.1 | async-start | bytes 2097152 | tf_op jit(solution)/shard_map/all_to_all | solution.py:187
  275.6 104.6 %copy-start.27 = (f32[1024]{0:T(1024)}, f32[1024]{0:T(1024)S(1)}, u32[]{:S(2)}) copy-start(f32[1024]{0:T(1024)S(1)} %convert_element_type.119) | copy-start | bytes 12292
  275.6 59.6 %copy-start.40 = (f32[1024]{0:T(1024)}, f32[1024]{0:T(1024)S(1)}, u32[]{:S(2)}) copy-start(f32[1024]{0:T(1024)S(1)} %convert_element_type.120) | copy-start | bytes 12292
  330.0 27.6 %copy-start.30 = (f32[32,1,128]{2,1,0:T(1,128)}, f32[32,1,128]{2,1,0:T(1,128)S(1)}, u32[]{:S(2)}) copy-start(f32[32,1,128]{2,1,0:T(1,128)S(1)} %convert_element_type.137) | copy-start | bytes 49156
  334.7 37.8 %copy-start.5 = (f32[512,1024]{1,0:T(8,128)}, f32[512,1024]{1,0:T(8,128)S(1)}, u32[]{:S(2)}) copy-start(f32[512,1024]{1,0:T(8,128)S(1)} %get-tuple-element.254) | copy-start | bytes 6291460
  334.7 45.5 %copy-start.19 = (f32[512]{0:T(512)}, f32[512]{0:T(512)S(1)}, u32[]{:S(2)}) copy-start(f32[512]{0:T(512)S(1)} %broadcast_multiply_fusion.4) | copy-start | bytes 6148
  335.1 45.1 %copy-start.32 = (f32[512]{0:T(512)}, f32[512]{0:T(512)S(1)}, u32[]{:S(2)}) copy-start(f32[512]{0:T(512)S(1)} %add_rsqrt_fusion) | copy-start | bytes 6148
  357.6 14.9 %copy-start.44 = (bf16[1024,4096]{1,0:T(8,128)(2,1)S(1)}, bf16[1024,4096]{1,0:T(8,128)(2,1)}, u32[]{:S(2)}) copy-start(bf16[1024,4096]{1,0:T(8,128)(2,1)} %all-gather.10.cloned.1.call-done) | copy-start | bytes 25165828
  372.5 7.7 copy-start.15
  383.6 9.2 copy-start.3
  385.9 27.0 %all-to-all-start.2 = ((bf16[512,4,256]{2,0,1:T(8,128)(2,1)}), bf16[512,4,256]{2,0,1:T(8,128)(2,1)}, u32[]{:S(2)}, u32[]{:S(2)}) async-start(bf16[512,4,256]{2,0,1:T(8,128)(2,1)} %bitcast.179), calls=%async_computation.2 | async-start | bytes 2097152 | tf_op jit(solution)/shard_map/all_to_all | solution.py:214
  390.4 414.4 %reduce-scatter.7.cloned.1.call-start = ((), (), s32[]{:S(2)}) async-start(), calls=%async_computation.13 | async-start | bytes 4325376 | tf_op jit(solution)/shard_map/reduce_scatter | solution.py:242
  397.2 455.8 %reduce-scatter.5.cloned.1.call-start = ((), (), s32[]{:S(2)}) async-start(), calls=%async_computation.12 | async-start | bytes 12976128 | tf_op jit(solution)/shard_map/reduce_scatter | solution.py:239
  416.9 5.1 copy-start.11
  420.9 5.3 copy-start.18
  443.9 7.0 copy-start
  455.0 5.0 copy-start.11
  459.0 5.3 copy-start.18
  482.4 7.0 copy-start
  494.1 5.0 copy-start.11
  498.1 5.3 copy-start.18
  521.5 6.9 copy-start
  533.2 5.0 copy-start.11
  537.2 5.3 copy-start.18
  560.6 6.9 copy-start
  682.9 4.8 copy-start.22
  682.9 4.8 copy-start.26
  682.9 4.8 copy-start.35
  683.0 4.8 copy-start.39
  696.5 345.6 %reduce-scatter.11.cloned.1.call-start = ((), (), s32[]{:S(2)}) async-start(), calls=%async_computation.15 | async-start | bytes 17301504 | tf_op jit(solution)/shard_map/reduce_scatter | solution.py:248
  714.0 515.6 %reduce-scatter.9.cloned.1.call-start = ((), (), s32[]{:S(2)}) async-start(), calls=%async_computation.14 | async-start | bytes 17301504 | tf_op jit(solution)/shard_map/reduce_scatter | solution.py:246
  727.8 13.2 %copy-start.10 = (bf16[512,3,4,256]{0,3,2,1:T(8,128)(2,1)S(1)}, bf16[512,3,4,256]{0,3,2,1:T(8,128)(2,1)}, u32[]{:S(2)}) copy-start(bf16[512,3,4,256]{0,3,2,1:T(8,128)(2,1)} %copy.84) | copy-start | bytes 9437188
  741.4 8.8 copy-start.23
  741.4 8.8 copy-start.24
  741.4 8.8 copy-start.29
  741.4 8.8 copy-start.36
  741.4 8.8 copy-start.37
  741.5 59.7 %copy-start.4 = (f32[512,1024]{1,0:T(8,128)S(1)}, f32[512,1024]{1,0:T(8,128)}, u32[]{:S(2)}) copy-start(f32[512,1024]{1,0:T(8,128)} %copy-done.3) | copy-start | bytes 6291460
  (26 other events, 79.3 us)
Sparse Core Ops, SparseCore 0:
  10.8 70.8 all-gather.5
  84.6 102.7 all-gather.7
  190.2 78.1 all-gather.9
  271.1 86.4 all-gather.11
  397.4 115.2 reduce-scatter.6
  696.6 156.3 reduce-scatter.4
  855.9 186.1 reduce-scatter.10
  1044.9 184.6 reduce-scatter.8
where the time goes:
time: 1250 us; the launch traced here: 1240 us
  waiting for transfers between devices  577 us (46%)
  matrix products  282 us (23%)
  blocking collectives  238 us (19%)
  local copies, waits for them, and re-layouts  70.1 us (6%)
  other arithmetic  22.6 us (2%)
  starting transfers between devices  17.6 us (1%)
  between operations  14.8 us (1%)
  loops' own time  14 us (1%)
    reduce_scatter x1, waiting for transfers between devices, per_device(): lax.psum_scatter(g_w_back, ('seq', 'shard'), scatter_dimension=0, tiled=T...  189 us
    reduce_scatter x1, waiting for transfers between devices, per_device(): lax.psum_scatter(g_w_in, ('seq', 'shard'), scatter_dimension=0, tiled=True)  188 us
    all_to_all x1, waiting for transfers between devices, per_device(): lax.all_to_all(qkv.reshape(rows, 3, width), 'seq', split_axis=2, concat_a...  101 us
    all_to_all x1, blocking collectives, per_device(): lax.all_to_all(stacked, 'seq', split_axis=0, concat_axis=2, tiled=True)  97.2 us
    unnamed x2, blocking collectives  86.4 us
    all_gather x1, blocking collectives, per_device(): lax.all_gather(bias_in, ('seq', 'shard'), axis=0, tiled=True)  54.4 us
    reduce_scatter x1, waiting for transfers between devices, per_device(): lax.psum_scatter(g_w_qkv, ('seq', 'shard'), scatter_dimension=0, tiled=True)  48.2 us
    dot_general x4, matrix products, one_block(): jnp.einsum('qgd,kgd->gqk', do_blk, values, preferred_element_type=jnp.flo...  42 us
  transfers between devices with their start and end apart: 11, of which 7 were waited for; matrix products, arithmetic and copies ran while one was open for 28% of the time, Pallas kernels for 0%

commit v1 on v0

--- a/solution.py
+++ b/solution.py
@@ -7,6 +7,13 @@
 HEAD_DIM = 64
 norm_eps = 1e-05
 gelu_c = math.sqrt(2.0 / math.pi)
+
+
+def swap_blocks(x, axis, split, join):
+    peers = lax.axis_size(axis)
+    pieces = jnp.stack(jnp.split(x, peers, axis=split), axis=0)
+    pieces = lax.all_to_all(pieces, axis, split_axis=0, concat_axis=0)
+    return jnp.concatenate(pieces, axis=join)
 
 
 def normalize(values):
@@ -174,9 +181,7 @@
     h_one = (normed1 * g_one.astype(f32) + s_one.astype(f32)).astype(jnp.bfloat16)
     bias_qkv = jnp.concatenate([full_bq.astype(f32), jnp.zeros((width,), f32), full_bv.astype(f32)])
     qkv = (jnp.dot(h_one, full_qkv, preferred_element_type=f32) + bias_qkv).astype(jnp.bfloat16)
-    grouped = lax.all_to_all(
-        qkv.reshape(rows, 3, width), "seq", split_axis=2, concat_axis=0, tiled=True
-    )
+    grouped = swap_blocks(qkv.reshape(rows, 3, width), "seq", 2, 0)
     length = grouped.shape[0]
     local_width = grouped.shape[2]
     groups = local_width // HEAD_DIM

time: 1250 us -> 1220 us (0.976)
  waiting for transfers between devices: 577 us -> 556 us
    all_to_all x1, waiting for transfers between devices: 101 us -> 75.9 us  [swap_blocks(): pieces = lax.all_to_all(pieces, axis, split_axis=0, concat_axis=0)]
where the time goes in v1:
time: 1220 us; the launch traced here: 1210 us
  waiting for transfers between devices  556 us (46%)
  matrix products  283 us (23%)
  blocking collectives  238 us (20%)
  local copies, waits for them, and re-layouts  62.6 us (5%)
  other arithmetic  24.5 us (2%)
  starting transfers between devices  15.3 us (1%)
  between operations  14.8 us (1%)
  loops' own time  14 us (1%)
    reduce_scatter x1, waiting for transfers between devices, per_device(): lax.psum_scatter(g_w_back, ('seq', 'shard'), scatter_dimension=0, tiled=T...  189 us
    reduce_scatter x1, waiting for transfers between devices, per_device(): lax.psum_scatter(g_w_in, ('seq', 'shard'), scatter_dimension=0, tiled=True)  188 us
    all_to_all x1, blocking collectives, per_device(): lax.all_to_all(stacked, 'seq', split_axis=0, concat_axis=2, tiled=True)  97.2 us
    unnamed x2, blocking collectives  86.5 us
    all_to_all x1, waiting for transfers between devices, swap_blocks(): pieces = lax.all_to_all(pieces, axis, split_axis=0, concat_axis=0)  75.9 us
    all_gather x1, blocking collectives, per_device(): lax.all_gather(bias_in, ('seq', 'shard'), axis=0, tiled=True)  54.7 us
    reduce_scatter x1, waiting for transfers between devices, per_device(): lax.psum_scatter(g_w_qkv, ('seq', 'shard'), scatter_dimension=0, tiled=True)  48.2 us
    dot_general x4, matrix products, one_block(): jnp.einsum('qgd,kgd->gqk', do_blk, values, preferred_element_type=jnp.flo...  42.1 us
  transfers between devices with their start and end apart: 11, of which 7 were waited for; matrix products, arithmetic and copies ran while one was open for 28% of the time, Pallas kernels for 0%

profile of v1, /device:TPU:13, one launch (start us, length us, event | category | flops | bytes accessed | tf_op | source)
XLA Modules:
  0.0 1208.5 jit_solution(5220360169140107189)
XLA Ops:
  16.1 40.8 %all-reduce.18 = (bf16[1024]{0:T(1024)(128)(2,1)S(1)}, bf16[1024]{0:T(1024)(128)(2,1)S(1)}, bf16[1024]{0:T(1024)(128)(2,1)S(1)}, bf16[1024]{0:T(1024)(128)(2,1)S...) all-reduce(bf16[1024]{0:T(1024)(128)(2,1)S(1)} %dynamic-update-slic, ...), channel_id=1, replica_groups=mesh['seq'=4,'shard'=8] {'seq','shard'}, use_global_device_ids=true, to_apply=%add.3 | all-reduce | flops 8192 | bytes 32768
  60.1 21.6 %all-gather.6.cloned.1.call-done = bf16[1024,3072]{1,0:T(8,128)(2,1)} async-done(((bf16[32,3072]{1,0:T(8,128)(2,1)}), bf16[1024,3072]{1,0:T(8,128)(2,1)}) %all-gather.6.cloned.1.call-update) | async-done | bytes 6291472 | tf_op jit(solution)/shard_map/all_gather | solution.py:150
  81.7 8.4 add_convert_fusion
  99.9 75.9 %all-to-all-done = bf16[4,512,3,256]{1,3,2,0:T(8,128)(2,1)S(1)} async-done(((bf16[4,512,3,256]{1,3,2,0:T(8,128)(2,1)}), bf16[4,512,3,256]{1,3,2,0:T(8,128)(2,1)S(1)}, u32[]{:S(2)}, u32[]{:S(2)}) %all-to-all-start) | async-done | bytes 3145760 | tf_op jit(solution)/shard_map/all_to_all | solution.py:15
  184.5 50.8 %while.27 = (s32[]{:T(128)}, bf16[4,512,4,64]{1,3,2,0:T(8,128)(2,1)}, f32[4,4,512]{2,1,0:T(4,128)}, s32[4]{0:T(128)S(1)}, bf16[2048,4,64]{0,2,1:T(8,128)(2,1)S(1...) while((s32[]{:T(128)}, ...), condition=%wide.region_4.5_spmd, body=%wide.region_2.4_spmd.sunk | while | flops 1104280064 | bytes 43569372 | solution.py:71
  186.4 4.7 exponential_reduce_fusion.2
  191.1 5.5 fusion.127
  199.1 4.7 exponential_reduce_fusion.2
  203.8 5.5 fusion.127
  211.8 4.7 exponential_reduce_fusion.2
  216.5 5.5 fusion.127
  224.5 4.7 exponential_reduce_fusion.2
  229.2 5.5 fusion.127
  236.3 6.3 all-to-all-start.1
  242.7 54.7 %all-gather = bf16[32,1,128]{2,1,0:T(2,128)(2,1)S(1)} all-gather(bf16[1,1,128]{2,1,0:T(2,128)(2,1)S(1)} %bitcast.192), channel_id=1, replica_groups=mesh['seq'=4,'shard'=8] {'seq','shard'}, dimensions={0}, use_global_device_ids=true | all-gather | bytes 8448 | tf_op jit(solution)/shard_map/all_gather | solution.py:158
  303.2 10.6 fusion.83
  313.8 15.4 %all-gather.12.cloned.1.call-done = bf16[4096,1024]{1,0:T(8,128)(2,1)} async-done(((bf16[128,1024]{1,0:T(8,128)(2,1)}), bf16[4096,1024]{1,0:T(8,128)(2,1)}) %all-gather.12.cloned.1.call-update) | async-done | bytes 8388624 | tf_op jit(solution)/shard_map/all_gather | solution.py:159
  329.2 15.0 %convert_reduce_fusion = (f32[4096]{0:T(1024)}, bf16[512,4096]{1,0:T(8,128)(2,1)}) fusion(f32[512,4096]{1,0:T(8,128)} %fusion.83, f32[4096]{0:T(1024)S(1)} %bitcast.189, bf16[4096,1024]{1,0:T(8,128)(2,1)} %all-gather.12.cloned.1.call-done, bf16[1,512,1024]{2,1,0:T(8,128)(2,1)} %param.33), kind=kOutput, calls=%fused_computation.52 | convolution fusion | flops 4341100544 | bytes 22052864 | tf_op jit(solution)/shard_map/dot_general | solution.py:124
  344.3 7.7 multiply_reduce_fusion.1
  369.1 15.7 %all-to-all-done.2 = bf16[512,4,256]{2,0,1:T(8,128)(2,1)} async-done(((bf16[512,4,256]{2,0,1:T(8,128)(2,1)}), bf16[512,4,256]{2,0,1:T(8,128)(2,1)}, u32[]{:S(2)}, u32[]{:S(2)}) %all-to-all-start.2) | async-done | bytes 1048608 | tf_op jit(solution)/shard_map/all_to_all | solution.py:219
  388.5 156.1 %while.28 = (s32[]{:T(128)}, f32[2048,4,64]{0,2,1:T(8,128)}, f32[2048,4,64]{0,2,1:T(8,128)}, bf16[4,512,4,64]{1,3,2,0:T(8,128)(2,1)}, s32[4]{0:T(128)S(1)}, /*in...) while((s32[]{:T(128)}, f32[2048,4,64]{0,2,1:T(8,128)}, ...), condition=%wide.region_11.12_spmd.clone, body=%wide.region_9.11_spmd.clone.sunk | while | flops 2734291456 | bytes 138236336 | solution.py:107
  398.0 7.2 fusion.140
  405.2 10.5 multiply_convert_fusion.5
  415.8 7.0 fusion.141
  436.1 7.6 fusion.140
  443.7 10.5 multiply_convert_fusion.5
  454.3 7.0 fusion.141
  461.2 4.8 fusion.139
  475.2 7.6 fusion.140
  482.9 10.5 multiply_convert_fusion.5
  493.4 6.9 fusion.141
  500.3 4.8 fusion.139
  514.4 7.6 fusion.140
  522.0 10.5 multiply_convert_fusion.5
  532.5 6.9 fusion.141
  539.4 4.8 fusion.139
  550.8 4.8 copy.80
  555.6 97.2 %all_to_all.55 = bf16[2048,3,256]{2,1,0:T(4,128)(2,1)S(1)} all-to-all(bf16[2048,3,256]{2,1,0:T(4,128)(2,1)} %copy.80), channel_id=1, replica_groups=mesh['seq'=4,'shard'=8] {'seq'}, dimensions={0} | all-to-all | bytes 6291456 | tf_op jit(solution)/shard_map/all_to_all | solution.py:231
  654.8 4.8 copy.82
  659.6 8.6 fusion.65
  669.5 16.2 %fusion.68 = f32[4096,1024]{1,0:T(8,128)} fusion(bf16[1,512,1024]{2,1,0:T(8,128)(2,1)S(1)} %copy-done.16, f32[512,4096]{1,0:T(8,128)} %fusion.83, f32[4096]{0:T(1024)S(1)} %bitcast.190), kind=kOutput, calls=%fused_computation.99 | convolution fusion | flops 4315938816 | bytes 26230784 | tf_op jit(solution)/shard_map/dot_general | solution.py:118
  687.4 11.5 fusion.82
  699.6 13.2 %fusion.63 = bf16[1,512,1024]{2,1,0:T(8,128)(2,1)} fusion(f32[512,1024]{1,0:T(8,128)S(1)} %copy-done.6, bf16[4096,1024]{1,0:T(8,128)(2,1)} %all-gather.12.cloned.1.call-done, f32[1024]{0:T(1024)S(1)} %convert_element_type.124, f32[512,4096]{1,0:T(8,128)} %fusion.83, f32[4096]{0:T(1024)S(1)} %bitcast.191), kind=kOutput, calls=%fused_computation.95 | convolution fusion | flops 4317511680 | bytes 19943424 | tf_op jit(solution)/shard_map/dot_general | solution.py:202
  713.3 8.8 fusion.56
  722.1 45.7 %all-reduce.17 = (f32[1024]{0:T(1024)S(1)}, f32[1024]{0:T(1024)S(1)}, f32[1024]{0:T(1024)S(1)}, f32[1024]{0:T(1024)S(1)}, f32[1024]{0:T(1024)S(1)}, /*index=5*/f...) all-reduce(f32[1024]{0:T(1024)S(1)} %get-tuple-element.184, ...), channel_id=2, replica_groups=mesh['seq'=4,'shard'=8] {'seq','shard'}, use_global_device_ids=true, to_apply=%region_15.16.clone | all-reduce | flops 12288 | bytes 98304
  776.7 48.2 %reduce-scatter.5.cloned.1.call-done = f32[32,3072]{1,0:T(8,128)} async-done(((f32[1024,3072]{1,0:T(8,128)}), f32[32,3072]{1,0:T(8,128)}) %reduce-scatter.5.cloned.1.call-update) | async-done | bytes 393232 | tf_op jit(solution)/shard_map/reduce_scatter | solution.py:244
  824.9 189.0 %reduce-scatter.11.cloned.1.call-done = f32[128,1024]{1,0:T(8,128)} async-done(((f32[4096,1024]{1,0:T(8,128)}), f32[128,1024]{1,0:T(8,128)}) %reduce-scatter.11.cloned.1.call-update) | async-done | bytes 524304 | tf_op jit(solution)/shard_map/reduce_scatter | solution.py:253
  1013.9 187.5 %reduce-scatter.9.cloned.1.call-done = f32[32,4096]{1,0:T(8,128)} async-done(((f32[1024,4096]{1,0:T(8,128)}), f32[32,4096]{1,0:T(8,128)}) %reduce-scatter.9.cloned.1.call-update) | async-done | bytes 524304 | tf_op jit(solution)/shard_map/reduce_scatter | solution.py:251
  (270 shorter events, 117.0 us)
Async XLA Ops:
  7.2 74.5 %all-gather.6.cloned.1.call-start = ((), (), s32[]{:S(2)}) async-start(), calls=%async_computation.8 | async-start | bytes 6488064 | tf_op jit(solution)/shard_map/all_gather | solution.py:150
  7.9 289.6 %all-gather.8.cloned.1.call-start = ((), (), s32[]{:S(2)}) async-start(), calls=%async_computation.9 | async-start | bytes 2162688 | tf_op jit(solution)/shard_map/all_gather | solution.py:153
  8.7 294.5 %all-gather.10.cloned.1.call-start = ((), (), s32[]{:S(2)}) async-start(), calls=%async_computation.10 | async-start | bytes 8650752 | tf_op jit(solution)/shard_map/all_gather | solution.py:157
  56.9 24.8 %copy-start.25 = (f32[1024]{0:T(1024)}, f32[1024]{0:T(1024)S(1)}, u32[]{:S(2)}) copy-start(f32[1024]{0:T(1024)S(1)} %convert_element_type.112) | copy-start | bytes 12292
  56.9 24.8 %copy-start.38 = (f32[1024]{0:T(1024)}, f32[1024]{0:T(1024)S(1)}, u32[]{:S(2)}) copy-start(f32[1024]{0:T(1024)S(1)} %convert_element_type.113) | copy-start | bytes 12292
  58.4 23.3 %copy-start.21 = (f32[512]{0:T(512)}, f32[512]{0:T(512)S(1)}, u32[]{:S(2)}) copy-start(f32[512]{0:T(512)S(1)} %broadcast_multiply_fusion.5) | copy-start | bytes 6148
  60.1 21.6 %copy-start.34 = (f32[512]{0:T(512)}, f32[512]{0:T(512)S(1)}, u32[]{:S(2)}) copy-start(f32[512]{0:T(512)S(1)} %add_rsqrt_fusion.1) | copy-start | bytes 6148
  95.4 80.3 %all-to-all-start = ((bf16[4,512,3,256]{1,3,2,0:T(8,128)(2,1)}), bf16[4,512,3,256]{1,3,2,0:T(8,128)(2,1)S(1)}, u32[]{:S(2)}, u32[]{:S(2)}) async-start(bf16[4,512,3,256]{1,3,2,0:T(8,128)(2,1)} %pad_maximum_fusion), calls=%async_computation | async-start | bytes 6291456 | tf_op jit(solution)/shard_map/all_to_all | solution.py:15
  99.3 229.9 %all-gather.12.cloned.1.call-start = ((), (), s32[]{:S(2)}) async-start(), calls=%async_computation.11 | async-start | bytes 8650752 | tf_op jit(solution)/shard_map/all_gather | solution.py:159
  184.5 58.2 %copy-start.43 = (bf16[128]{0:T(256)(128)(2,1)S(1)}, bf16[128]{0:T(256)(128)(2,1)}, u32[]{:S(2)}) copy-start(bf16[128]{0:T(256)(128)(2,1)} %param.30) | copy-start | bytes 772
  236.3 61.2 %all-to-all-start.1 = ((bf16[4,512,256]{1,2,0:T(8,128)(2,1)}), bf16[4,512,256]{1,2,0:T(8,128)(2,1)S(1)}, u32[]{:S(2)}, u32[]{:S(2)}) async-start(bf16[4,512,256]{1,2,0:T(8,128)(2,1)} %bitcast.14), calls=%async_computation.1 | async-start | bytes 2097152 | tf_op jit(solution)/shard_map/all_to_all | solution.py:192
  242.6 109.3 %copy-start.27 = (f32[1024]{0:T(1024)}, f32[1024]{0:T(1024)S(1)}, u32[]{:S(2)}) copy-start(f32[1024]{0:T(1024)S(1)} %convert_element_type.119) | copy-start | bytes 12292
  242.7 60.5 %copy-start.40 = (f32[1024]{0:T(1024)}, f32[1024]{0:T(1024)S(1)}, u32[]{:S(2)}) copy-start(f32[1024]{0:T(1024)S(1)} %convert_element_type.120) | copy-start | bytes 12292
  297.4 31.8 %copy-start.30 = (f32[32,1,128]{2,1,0:T(1,128)}, f32[32,1,128]{2,1,0:T(1,128)S(1)}, u32[]{:S(2)}) copy-start(f32[32,1,128]{2,1,0:T(1,128)S(1)} %convert_element_type.137) | copy-start | bytes 49156
  302.8 41.5 %copy-start.5 = (f32[512,1024]{1,0:T(8,128)}, f32[512,1024]{1,0:T(8,128)S(1)}, u32[]{:S(2)}) copy-start(f32[512,1024]{1,0:T(8,128)S(1)} %get-tuple-element.258) | copy-start | bytes 6291460
  302.8 49.2 %copy-start.19 = (f32[512]{0:T(512)}, f32[512]{0:T(512)S(1)}, u32[]{:S(2)}) copy-start(f32[512]{0:T(512)S(1)} %broadcast_multiply_fusion.4) | copy-start | bytes 6148
  303.1 48.8 %copy-start.32 = (f32[512]{0:T(512)}, f32[512]{0:T(512)S(1)}, u32[]{:S(2)}) copy-start(f32[512]{0:T(512)S(1)} %add_rsqrt_fusion) | copy-start | bytes 6148
  329.2 15.0 %copy-start.44 = (bf16[1024,4096]{1,0:T(8,128)(2,1)S(1)}, bf16[1024,4096]{1,0:T(8,128)(2,1)}, u32[]{:S(2)}) copy-start(bf16[1024,4096]{1,0:T(8,128)(2,1)} %all-gather.10.cloned.1.call-done) | copy-start | bytes 25165828
  344.3 7.7 copy-start.15
  355.4 9.2 copy-start.3
  357.8 27.0 %all-to-all-start.2 = ((bf16[512,4,256]{2,0,1:T(8,128)(2,1)}), bf16[512,4,256]{2,0,1:T(8,128)(2,1)}, u32[]{:S(2)}, u32[]{:S(2)}) async-start(bf16[512,4,256]{2,0,1:T(8,128)(2,1)} %bitcast.183), calls=%async_computation.2 | async-start | bytes 2097152 | tf_op jit(solution)/shard_map/all_to_all | solution.py:219
  362.2 414.5 %reduce-scatter.7.cloned.1.call-start = ((), (), s32[]{:S(2)}) async-start(), calls=%async_computation.13 | async-start | bytes 4325376 | tf_op jit(solution)/shard_map/reduce_scatter | solution.py:247
  369.1 455.9 %reduce-scatter.5.cloned.1.call-start = ((), (), s32[]{:S(2)}) async-start(), calls=%async_computation.12 | async-start | bytes 12976128 | tf_op jit(solution)/shard_map/reduce_scatter | solution.py:244
  388.7 5.0 copy-start.11
  392.7 5.3 copy-start.18
  415.8 7.0 copy-start
  426.8 5.0 copy-start.11
  430.8 5.3 copy-start.18
  454.3 7.0 copy-start
  466.0 5.0 copy-start.11
  469.9 5.3 copy-start.18
  493.4 6.9 copy-start
  505.1 5.0 copy-start.11
  509.1 5.3 copy-start.18
  532.5 6.9 copy-start
  654.8 4.8 copy-start.22
  654.8 4.8 copy-start.26
  654.8 4.8 copy-start.35
  654.8 4.8 copy-start.39
  668.3 345.7 %reduce-scatter.11.cloned.1.call-start = ((), (), s32[]{:S(2)}) async-start(), calls=%async_computation.15 | async-start | bytes 17301504 | tf_op jit(solution)/shard_map/reduce_scatter | solution.py:253
  685.8 515.7 %reduce-scatter.9.cloned.1.call-start = ((), (), s32[]{:S(2)}) async-start(), calls=%async_computation.14 | async-start | bytes 17301504 | tf_op jit(solution)/shard_map/reduce_scatter | solution.py:251
  699.6 13.2 %copy-start.10 = (bf16[512,3,4,256]{0,3,2,1:T(8,128)(2,1)S(1)}, bf16[512,3,4,256]{0,3,2,1:T(8,128)(2,1)}, u32[]{:S(2)}) copy-start(bf16[512,3,4,256]{0,3,2,1:T(8,128)(2,1)} %copy.82) | copy-start | bytes 9437188
  713.2 8.8 copy-start.23
  713.2 8.8 copy-start.24
  713.2 8.8 copy-start.29
  713.2 8.8 copy-start.36
  713.2 8.8 copy-start.37
  713.3 59.8 %copy-start.4 = (f32[512,1024]{1,0:T(8,128)S(1)}, f32[512,1024]{1,0:T(8,128)}, u32[]{:S(2)}) copy-start(f32[512,1024]{1,0:T(8,128)} %copy-done.3) | copy-start | bytes 6291460
  (26 other events, 79.0 us)
Sparse Core Ops, SparseCore 0:
  10.8 70.8 all-gather.5
  84.6 82.3 all-gather.7
  169.8 75.5 all-gather.9
  248.1 81.0 all-gather.11
  369.2 115.2 reduce-scatter.6
  668.4 156.4 reduce-scatter.4
  827.8 186.1 reduce-scatter.10
  1016.8 184.6 reduce-scatter.8
